TPU v7x, 32 devices: a whole 2x2x4 slice. The times are simulated.
32 devices in a mesh: clip: 2 (over y), ha: 4 (over z), wa: 4 (over x, core).
Axes of the slice: x: 2, y: 2, z: 4, core: 2. Of those that a mesh axis runs over, the one named last changes fastest.
Arguments:
- cotangent: float32 [8, 16, 256, 96], P('clip', 'ha', 'wa'), parts along dimension 0, may hold values from -6 to 6
- stored_first: float32 [8, 16, 256, 96], P('clip', 'ha', 'wa'), parts along dimension 0, may hold values from -8 to 8
- stored_second: float32 [8, 16, 256, 96], P('clip', 'ha', 'wa'), parts along dimension 0, may hold values from -8 to 8
- w_first: float32 [3, 3, 3, 96, 96], replicated, may hold values from -0.125 to 0.125
- w_second: float32 [3, 3, 3, 96, 96], replicated, may hold values from -0.125 to 0.125
- w_third: float32 [3, 3, 3, 96, 96], replicated, may hold values from -0.125 to 0.125
Outputs:
- input_grad: float32 [8, 16, 256, 96], P('clip', 'ha', 'wa'), parts along dimension 0
There are 2 independent parts, one for each index of `clip`. A program takes and returns all parts, laid end to end along the dimension named above; an argument that names none is the same for every part. Nothing has to cross between parts.
All inputs are finite; a program needn't handle non-finite values.
Results may differ from a plain program's by a relative error of at most 0.00013.
Values sent between devices are 32-bit elements; how exact they have to be, the bound alone decides.
A program may use at most 64 MiB of HBM per device.

v0:
```python
import functools

import jax
import jax.numpy as jnp
from jax import lax
from jax.experimental import pallas as pl
from jax.experimental.pallas import tpu as pltpu
from jax.sharding import PartitionSpec as P

LANES = 128
EDGE = 8
SIDES = tuple((dh, dw) for dh in (-1, 0, 1) for dw in (-1, 0, 1) if (dh, dw) != (0, 0))
COLS = ((0, -1), (0, 1))
ROWS = tuple(s for s in SIDES if s[0] != 0)


def silu_slope(value):
    sigma = 1.0 / (1.0 + jnp.exp(-value))
    return sigma * (1.0 + value * (1.0 - sigma))


def split(value):
    high = value.astype(jnp.bfloat16)
    low = (value - high.astype(jnp.float32)).astype(jnp.bfloat16)
    return high, low


def kernel(
    sizes, cot, first, second, w1, w2, w3, out,
    ext0, ext1, ext2, xs, wbuf0, wbuf1, wbuf2, whl, acc, sfirst, ssecond,
    local_sem, send_sem, recv_sem,
):
    nh, nw, F, R, W, C = sizes
    span = 3 * LANES
    exts = (ext0, ext1, ext2)
    wbufs = (wbuf0, wbuf1, wbuf2)
    ih, iw = lax.axis_index("ha"), lax.axis_index("wa")

    def present(dh, dw):
        ok = ih >= 0
        if dh:
            ok = ok & ((ih > 0) if dh < 0 else (ih < nh - 1))
        if dw:
            ok = ok & ((iw > 0) if dw < 0 else (iw < nw - 1))
        return ok

    def one(flag):
        return jnp.where(flag, jnp.int32(1), jnp.int32(0))

    loads = [
        pltpu.make_async_copy(cot, ext0.at[:, pl.ds(1, R), pl.ds(EDGE, W), :], local_sem.at[0]),
        pltpu.make_async_copy(w3, wbuf0, local_sem.at[1]),
        pltpu.make_async_copy(w2, wbuf1, local_sem.at[2]),
        pltpu.make_async_copy(w1, wbuf2, local_sem.at[3]),
        pltpu.make_async_copy(second, ssecond, local_sem.at[4]),
        pltpu.make_async_copy(first, sfirst, local_sem.at[5]),
    ]
    for load in loads:
        load.start()

    barrier = pltpu.get_barrier_semaphore()
    for dh, dw in SIDES:
        @pl.when(present(dh, dw))
        def _():
            pl.semaphore_signal(
                barrier, inc=1, device_id={"ha": ih + dh, "wa": iw + dw},
                device_id_type=pl.DeviceIdType.MESH,
            )
    tall = 1 + one(ih > 0) + one(ih < nh - 1)
    wide = 1 + one(iw > 0) + one(iw < nw - 1)
    pl.semaphore_wait(barrier, tall * wide - 1)

    groups = ((F // 2, F), (0, F // 2))

    def copy_to(phase, group, dh, dw):
        t0, t1 = groups[group]
        row, rows = {-1: (0, 1), 0: (0, R), 1: (R - 1, 1)}[dh]
        col, cols = {-1: (0, EDGE), 0: (0, W), 1: (W - EDGE, EDGE)}[dw]
        drow = {-1: R + 1, 0: 1, 1: 0}[dh]
        dcol = {-1: EDGE + W, 0: EDGE, 1: 0}[dw]
        ext, frames = exts[phase], pl.ds(t0, t1 - t0)
        if phase == 0:
            src = cot.at[frames, pl.ds(row, rows), pl.ds(col, cols), :]
        else:
            src = ext.at[frames, pl.ds(row + 1, rows), pl.ds(col + EDGE, cols), :]
        at = SIDES.index((dh, dw))
        return pltpu.make_async_remote_copy(
            src_ref=src,
            dst_ref=ext.at[frames, pl.ds(drow, rows), pl.ds(dcol, cols), :],
            send_sem=send_sem.at[phase, group, at],
            recv_sem=recv_sem.at[phase, group, at],
            device_id={"ha": ih + dh, "wa": iw + dw},
            device_id_type=pl.DeviceIdType.MESH,
        )

    def send(phase, group):
        for dh, dw in COLS + ROWS:
            @pl.when(present(dh, dw))
            def _():
                copy_to(phase, group, dh, dw).start()

    def receive(phase, group, sides):
        for dh, dw in sides:
            @pl.when(present(-dh, -dw))
            def _():
                copy_to(phase, group, dh, dw).wait_recv()

    send(0, 0)
    send(0, 1)

    xs[...] = jnp.zeros_like(xs)
    for dh, dw in SIDES:
        @pl.when(jnp.logical_not(present(dh, dw)))
        def _():
            row, rows = {-1: (0, 1), 0: (1, R), 1: (R + 1, 1)}[dh]
            col, cols = {-1: (0, EDGE), 0: (EDGE, W), 1: (EDGE + W, EDGE)}[dw]
            for ext in exts:
                ext[:, row : row + rows, col : col + cols, :] = jnp.zeros(
                    (F, rows, cols, C), jnp.float32
                )

    def prepare(phase):
        wbuf = wbufs[phase]

        @pl.loop(0, 3)
        def _(i):
            for j in range(3):
                for k in range(3):
                    turned = split(jnp.transpose(wbuf[i, j, k]))
                    for part in range(2):
                        at = part * span + k * LANES
                        whl[phase, i, j, at : at + C, 0:C] = turned[part]
                        whl[phase, i, j, at + C : at + LANES, :] = jnp.zeros(
                            (LANES - C, LANES), jnp.bfloat16
                        )

    def arrange(phase, group, rows):
        ext = exts[phase]

        @pl.loop(*groups[group])
        def _(f):
            for e in rows:
                for k in range(3):
                    start = EDGE + 1 - k
                    high, low = split(ext[f, e, start : start + W, :])
                    xs[f, e, :, k * LANES : k * LANES + C] = high
                    xs[f, e, :, span + k * LANES : span + k * LANES + C] = low

    pairs = R // 2

    def reach(group, i):
        t0, t1 = groups[group]
        return t0, min(t1, F - 2 + i)

    def lhs(group, i, q):
        t0, t1 = reach(group, i)
        parts = [xs[t0 + 2 - i : t1 + 2 - i, 2 * p + q][:, None] for p in range(pairs)]
        block = jnp.concatenate(parts, axis=1).reshape((t1 - t0) * pairs * W, 2 * span)
        return jnp.concatenate([block, block[:, :span]], axis=1)

    def rhs(phase, i, j):
        high, low = whl[phase, i, j, :span], whl[phase, i, j, span:]
        return jnp.concatenate([high, high, low], axis=0)

    def dot(a, b):
        return jnp.dot(a, b, preferred_element_type=jnp.float32)

    def weights(phase, i, j):
        if 0 <= j <= 2:
            return rhs(phase, i, j)
        return jnp.zeros((3 * span, LANES), jnp.bfloat16)

    def multiply(phase, group, offsets, fresh):
        for i in (2, 1, 0):
            t0, t1 = reach(group, i)
            if t1 <= t0:
                continue
            a = jnp.concatenate([lhs(group, i, q) for q in offsets], axis=1)
            b = jnp.concatenate(
                [
                    jnp.concatenate([weights(phase, i, 2 - q), weights(phase, i, 3 - q)], axis=1)
                    for q in offsets
                ],
                axis=0,
            )
            value = dot(a, b).reshape(t1 - t0, pairs, W, 2 * LANES)
            if fresh and i == 2:
                acc[t0:t1] = value
            else:
                acc[t0:t1] += value

    for phase in range(3):
        loads[phase + 1].wait()
        prepare(phase)
    loads[0].wait()
    for phase in range(3):
        for group in range(2):
            t0, t1 = groups[group]
            if phase and group == 0:
                receive(phase, group, SIDES)
                arrange(phase, group, range(R + 2))
                multiply(phase, group, (0, 1, 2, 3), True)
            else:
                receive(phase, group, COLS)
                arrange(phase, group, range(1, R + 1))
                multiply(phase, group, (1, 2), True)
                receive(phase, group, ROWS)
                arrange(phase, group, (0, R + 1))
                multiply(phase, group, (0, 3), False)
            if phase < 2 and group == 0:
                loads[4 + phase].wait()
            for h in range(R):
                at = h % 2 * LANES
                value = acc[t0:t1, h // 2, :, at : at + C]
                if phase < 2:
                    stored = (ssecond, sfirst)[phase]
                    exts[phase + 1][t0:t1, h + 1, EDGE : EDGE + W, :] = value * silu_slope(
                        stored[t0:t1, h]
                    )
                else:
                    out[t0:t1, h] = value
            if phase < 2:
                send(phase + 1, group)

    for phase in range(3):
        for group in range(2):
            for dh, dw in SIDES:
                @pl.when(present(dh, dw))
                def _():
                    copy_to(phase, group, dh, dw).wait_send()


def local(cotangent, stored_first, stored_second, w_first, w_second, w_third):
    F, R, W, C = cotangent.shape
    sizes = (lax.axis_size("ha"), lax.axis_size("wa"), F, R, W, C)
    ext = pltpu.VMEM((F, R + 2, W + 2 * EDGE, C), jnp.float32)
    wbuf = pltpu.VMEM(w_first.shape, jnp.float32)
    stored = pltpu.VMEM((F, R, W, C), jnp.float32)
    return pl.pallas_call(
        functools.partial(kernel, sizes),
        out_shape=jax.ShapeDtypeStruct(cotangent.shape, jnp.float32),
        in_specs=[pl.BlockSpec(memory_space=pltpu.HBM)] * 6,
        out_specs=pl.BlockSpec(memory_space=pltpu.VMEM),
        scratch_shapes=[
            ext, ext, ext,
            pltpu.VMEM((F, R + 2, W, 6 * LANES), jnp.bfloat16),
            wbuf, wbuf, wbuf,
            pltpu.VMEM((3, 3, 3, 6 * LANES, LANES), jnp.bfloat16),
            pltpu.VMEM((F, R // 2, W, 2 * LANES), jnp.float32),
            stored, stored,
            pltpu.SemaphoreType.DMA((6,)),
            pltpu.SemaphoreType.DMA((3, 2, 8)),
            pltpu.SemaphoreType.DMA((3, 2, 8)),
        ],
        compiler_params=pltpu.CompilerParams(
            collective_id=0, has_side_effects=True, vmem_limit_bytes=67043328
        ),
    )(cotangent, stored_first, stored_second, w_first, w_second, w_third)


def solution(mesh):
    split_spec = P("clip", "ha", "wa", None)
    return jax.shard_map(
        local,
        mesh=mesh,
        in_specs=(split_spec, split_spec, split_spec, P(), P(), P()),
        out_specs=split_spec,
        check_vma=False,
    )
```

profile of v0, /device:TPU:1, one launch (start us, length us, event | category | flops | bytes accessed | tf_op | source)
XLA Modules:
  0.0 28.6 jit_solution(9462631968654528310)
XLA Ops:
  0.0 26.7 %shard_map.64 = f32[4,4,64,96]{3,2,1,0:T(8,128)} custom-call(f32[4,4,64,96]{3,2,1,0:T(8,128)} %cot.1, f32[4,4,64,96]{3,2,1,0:T(8,128)} %first.1, f32[4,4,64,96]{3,2,1,0:T(8,128)} %second.1, f32[3,3,3,96,96]{4,3,2,1,0:T(8,128)} %w1.1, f32[3,3,3,96,96]{4,3,2,1,0:T(8,128)} %w2.1, f32[3,3,3,96,96]{4,3,2,1,0:T(8,128)} %w3.1), custom_call_target="tpu_custom_call" | custom-call | tf_op jit(solution)/shard_map/pallas_call | solution.py:239
  26.7 1.9 %copy.8 = f32[4,4,64,96]{3,2,1,0:T(8,128)} copy(f32[4,4,64,96]{3,2,1,0:T(8,128)} %shard_map.64) | data formatting | bytes 786432
where the time goes:
time: 28.7 us; the launch traced here: 28.6 us
  Pallas kernels  26.7 us (93%)
  local copies, waits for them, and re-layouts  1.89 us (7%)
    pallas_call x1, Pallas kernels, local(): pl.pallas_call(functools.partial(kernel, sizes), out_shape=jax.ShapeDtype...  26.7 us
    unnamed x1, local copies, waits for them, and re-layouts  1.89 us

commit v1 on v0

--- a/solution.py
+++ b/solution.py
@@ -238,7 +238,7 @@
     stored = pltpu.VMEM((F, R, W, C), jnp.float32)
     return pl.pallas_call(
         functools.partial(kernel, sizes),
-        out_shape=jax.ShapeDtypeStruct(cotangent.shape, jnp.float32),
+        out_shape=pltpu.VMEM(cotangent.shape, jnp.float32),
         in_specs=[pl.BlockSpec(memory_space=pltpu.HBM)] * 6,
         out_specs=pl.BlockSpec(memory_space=pltpu.VMEM),
         scratch_shapes=[
@@ -253,7 +253,7 @@
             pltpu.SemaphoreType.DMA((3, 2, 8)),
         ],
         compiler_params=pltpu.CompilerParams(
-            collective_id=0, has_side_effects=True, vmem_limit_bytes=67043328
+            collective_id=0, has_side_effects=True, vmem_limit_bytes=67043328 - cotangent.size * 6
         ),
     )(cotangent, stored_first, stored_second, w_first, w_second, w_third)
 

time: 28.7 us -> 26.9 us (0.937)
  local copies, waits for them, and re-layouts: 1.89 us -> 0.8 us
  Pallas kernels: 26.7 us -> 25.9 us
    unnamed x1, local copies, waits for them, and re-layouts: 1.89 us -> 0.8 us
    pallas_call x1, Pallas kernels: 26.7 us -> 25.9 us  [local(): pl.pallas_call(functools.partial(kernel, sizes), out_shape=pltpu.VMEM(cot...]
where the time goes in v1:
time: 26.9 us; the launch traced here: 26.7 us
  Pallas kernels  25.9 us (96%)
  local copies, waits for them, and re-layouts  0.8 us (3%)
    pallas_call x1, Pallas kernels, local(): pl.pallas_call(functools.partial(kernel, sizes), out_shape=pltpu.VMEM(cot...  25.9 us
    unnamed x1, local copies, waits for them, and re-layouts  0.8 us

profile of v1, /device:TPU:1, one launch (start us, length us, event | category | flops | bytes accessed | tf_op | source)
XLA Modules:
  0.0 26.7 jit_solution(373544756329382521)
XLA Ops:
  0.0 25.9 %shard_map.64 = f32[4,4,64,96]{3,2,1,0:T(8,128)S(1)} custom-call(f32[4,4,64,96]{3,2,1,0:T(8,128)} %cot.1, f32[4,4,64,96]{3,2,1,0:T(8,128)} %first.1, f32[4,4,64,96]{3,2,1,0:T(8,128)} %second.1, f32[3,3,3,96,96]{4,3,2,1,0:T(8,128)} %w1.1, f32[3,3,3,96,96]{4,3,2,1,0:T(8,128)} %w2.1, f32[3,3,3,96,96]{4,3,2,1,0:T(8,128)} %w3.1), custom_call_target="tpu_custom_call" | custom-call | tf_op jit(solution)/shard_map/pallas_call | solution.py:239
  25.9 0.8 %copy.8 = f32[4,4,64,96]{3,2,1,0:T(8,128)} copy(f32[4,4,64,96]{3,2,1,0:T(8,128)S(1)} %shard_map.64) | data formatting | bytes 786432

commit v2 on v1

v2 whole, which is shorter than its diff:
```python
import functools

import jax
import jax.numpy as jnp
from jax import lax
from jax.experimental import pallas as pl
from jax.experimental.pallas import tpu as pltpu
from jax.sharding import PartitionSpec as P

LANES = 128
NB = 4
SIDES = tuple((dh, dw) for dh in (-1, 0, 1) for dw in (-1, 0, 1) if (dh, dw) != (0, 0))
CORNERS = tuple(s for s in SIDES if s[0] and s[1])
COLS = ((0, -1), (0, 1))
ROWS = ((-1, 0), (1, 0))
ORDER = CORNERS + COLS + ROWS


def silu_slope(value):
    sigma = 1.0 / (1.0 + jnp.exp(-value))
    return sigma * (1.0 + value * (1.0 - sigma))


def split(value):
    high = value.astype(jnp.bfloat16)
    low = (value - high.astype(jnp.float32)).astype(jnp.bfloat16)
    return high, low


def kernel(
    sizes, cot, first, second, w1, w2, w3, out,
    vcot, sfirst, ssecond, slopes, wbuf0, wbuf1, wbuf2, wh, own, lhs, acc,
    zsend, zrecv, xsend, xrecv, crecv,
    local_sem, send_sem, recv_sem,
):
    nh, nw, F, R, W, C = sizes
    A, pairs = W // NB, R // 2
    rows = NB * pairs * A
    wbufs = (wbuf0, wbuf1, wbuf2)
    ih, iw = lax.axis_index("ha"), lax.axis_index("wa")

    def present(dh, dw):
        ok = ih >= 0
        if dh:
            ok = ok & ((ih > 0) if dh < 0 else (ih < nh - 1))
        if dw:
            ok = ok & ((iw > 0) if dw < 0 else (iw < nw - 1))
        return ok

    def one(flag):
        return jnp.where(flag, jnp.int32(1), jnp.int32(0))

    barrier = pltpu.get_barrier_semaphore()
    for dh, dw in SIDES:
        @pl.when(present(dh, dw))
        def _():
            pl.semaphore_signal(
                barrier, inc=1, device_id={"ha": ih + dh, "wa": iw + dw},
                device_id_type=pl.DeviceIdType.MESH,
            )

    loads = [
        pltpu.make_async_copy(cot, vcot, local_sem.at[0]),
        pltpu.make_async_copy(w3, wbuf0, local_sem.at[1]),
        pltpu.make_async_copy(second, ssecond, local_sem.at[4]),
        pltpu.make_async_copy(w2, wbuf1, local_sem.at[2]),
        pltpu.make_async_copy(first, sfirst, local_sem.at[5]),
        pltpu.make_async_copy(w1, wbuf2, local_sem.at[3]),
    ]
    for load in loads:
        load.start()

    def side(d):
        return (d + 1) // 2

    def landing(phase, t, dh, dw):
        if dh and dw:
            return crecv.at[phase, t, side(dh), side(dw)]
        if dw:
            return xrecv.at[phase, t, side(dw)]
        return zrecv.at[phase, t, side(dh)]

    def copy_to(phase, t, dh, dw):
        at = SIDES.index((dh, dw))
        source = xsend.at[phase, t, side(dw)] if dw else zsend.at[phase, t, side(dh)]
        return pltpu.make_async_remote_copy(
            src_ref=source,
            dst_ref=landing(phase, t, -dh, -dw),
            send_sem=send_sem.at[phase, t, at],
            recv_sem=recv_sem.at[phase, t, at],
            device_id={"ha": ih + dh, "wa": iw + dw},
            device_id_type=pl.DeviceIdType.MESH,
        )

    def send(phase, t):
        for dh, dw in ORDER:
            @pl.when(present(dh, dw))
            def _():
                copy_to(phase, t, dh, dw).start()

    def receive(phase, t):
        for dh, dw in ORDER:
            @pl.when(present(-dh, -dw))
            def _():
                copy_to(phase, t, dh, dw).wait_recv()

    for dh, dw in SIDES:
        @pl.when(jnp.logical_not(present(dh, dw)))
        def _():
            for phase in range(3):
                for t in range(F):
                    ref = landing(phase, t, dh, dw)
                    ref[...] = jnp.zeros(ref.shape, jnp.float32)

    lane = lax.broadcasted_iota(jnp.int32, (A, LANES), 1)
    line = lax.broadcasted_iota(jnp.int32, (A, LANES), 0)
    real = lane < C
    third = C // 3

    def wide(value):
        return jnp.concatenate(
            [value, jnp.zeros((value.shape[0], LANES - C), jnp.float32)], axis=1
        )

    def place(b, r):
        return (b * pairs + r // 2) * A

    def post(phase, t, tile):
        for r, to in ((0, 0), (R - 1, 1)):
            last = tile(r, NB - 1)
            for m in range(3):
                moved = pltpu.roll(last, LANES - third - third * m, axis=1)
                zsend[phase, t, to, m * A : (m + 1) * A, :] = jnp.where(real, tile(r, m), moved)
        for r in range(R):
            xsend[phase, t, 0, r : r + 1, :] = tile(r, 0)[0:1]
            xsend[phase, t, 1, r : r + 1, :] = tile(r, NB - 1)[A - 1 : A]

    def unpack(phase, t, to):
        packed = [zrecv[phase, t, to, m * A : (m + 1) * A, :] for m in range(3)]
        moved = [pltpu.roll(packed[m], third + third * m, axis=1) for m in range(3)]
        last = jnp.where(lane < third, moved[0], jnp.where(lane < 2 * third, moved[1], moved[2]))
        return [jnp.where(real, v, 0.0) for v in packed + [last]]

    xsend[...] = jnp.zeros_like(xsend)
    loads[0].wait()

    for t in reversed(range(F)):
        tiles = {}
        for r in range(R):
            for b in range(NB):
                tiles[r, b] = wide(vcot[t, r, pl.ds(b, A, stride=NB), :])
                own[0, t, r % 2, place(b, r) : place(b, r) + A, :] = tiles[r, b]
        post(0, t, lambda r, b: tiles[r, b])

    tall = 1 + one(ih > 0) + one(ih < nh - 1)
    broad = 1 + one(iw > 0) + one(iw < nw - 1)
    pl.semaphore_wait(barrier, tall * broad - 1)
    for t in reversed(range(F)):
        send(0, t)

    def prepare(phase):
        wbuf = wbufs[phase]

        @pl.loop(0, 3)
        def _(i):
            for k in range(3):
                g0, g1, g2 = (wide(wbuf[i, 2 - e, k]) for e in range(3))
                even, odd = (g0 + g2) * 0.5, g1 * 0.5
                for q, value in enumerate((g0, even + odd, even - odd, g2)):
                    high, low = split(value)
                    at = k * LANES
                    wh[phase, i, q, 0:C, at : at + LANES] = high
                    wh[phase, i, q, LANES : LANES + C, at : at + LANES] = low

    def slope_of(stored, at):
        @pl.loop(0, F)
        def _(t):
            for r in range(R):
                for b in range(NB):
                    slopes[at, t, r % 2, place(b, r) : place(b, r) + A, :] = wide(
                        silu_slope(stored[t, r, pl.ds(b, A, stride=NB), :])
                    )

    loads[1].wait()
    prepare(0)
    loads[2].wait()
    slope_of(ssecond, 0)
    loads[3].wait()
    prepare(1)
    loads[4].wait()
    slope_of(sfirst, 1)
    loads[5].wait()
    prepare(2)

    def arrange(phase, t):
        tiles = {}
        for r in range(-1, R + 1):
            if 0 <= r < R:
                for b in range(NB):
                    tiles[r, b] = own[phase, t, r % 2, place(b, r) : place(b, r) + A, :]
                left, right = (xrecv[phase, t, s, r : r + 1, :] for s in range(2))
            else:
                to = 0 if r < 0 else 1
                for b, value in enumerate(unpack(phase, t, to)):
                    tiles[r, b] = value
                near = R - 1 if r < 0 else 0
                left, right = (crecv[phase, t, to, s, near : near + 1, :] for s in range(2))
            tiles[r, -1] = jnp.where(line == 0, left, pltpu.roll(tiles[r, NB - 1], 1, axis=0))
            tiles[r, NB] = jnp.where(line == A - 1, right, pltpu.roll(tiles[r, 0], A - 1, axis=0))
        for p in range(pairs):
            for b in range(-1, NB + 1):
                d0, d1, d2, d3 = (tiles[2 * p - 1 + n, b] for n in range(4))
                for q, value in enumerate((d0 - d2, d1 + d2, d2 - d1, d1 - d3)):
                    high, low = split(value)
                    lhs[t, q, b + 1, p * A : (p + 1) * A, 0:LANES] = high
                    lhs[t, q, b + 1, p * A : (p + 1) * A, LANES:] = low

    def product(phase, t, i, q):
        a = jnp.concatenate(
            [lhs[t, q, 2 - k : 2 - k + NB].reshape(rows, 2 * LANES) for k in range(3)], axis=1
        )
        w = [wh[phase, i, q, :, k * LANES : (k + 1) * LANES] for k in range(3)]
        b = jnp.concatenate([w[0], w[0], w[1], w[1], w[2], w[2]], axis=1)
        value = lax.dot_general(
            a, b, (((1,), (1,)), ((), ())), preferred_element_type=jnp.float32
        )
        return value[:, :LANES] + value[:, LANES:]

    allreal = lax.broadcasted_iota(jnp.int32, (rows, LANES), 1) < C

    for phase in range(3):
        for t in reversed(range(F)):
            receive(phase, t)
            arrange(phase, t)
            m = []
            for q in range(4):
                value = product(phase, t, 2, q)
                m.append(value if t == F - 1 else value + acc[t, q])
            done = (m[0] + m[1] + m[2], m[1] - m[2] - m[3])
            if phase < 2:
                done = [jnp.where(allreal, done[s] * slopes[phase, t, s], 0.0) for s in range(2)]
                for s in range(2):
                    own[phase + 1, t, s] = done[s]
                post(phase + 1, t, lambda r, b: done[r % 2][place(b, r) : place(b, r) + A])
                send(phase + 1, t)
            else:
                for r in range(R):
                    for b in range(NB):
                        out[t, r, pl.ds(b, A, stride=NB), :] = done[r % 2][
                            place(b, r) : place(b, r) + A, :C
                        ]
            for back in (1, 2):
                if t - back >= 0:
                    for q in range(4):
                        value = product(phase, t, 2 - back, q)
                        if t + 1 < F and back == 1:
                            acc[t - 1, q] += value
                        else:
                            acc[t - back, q] = value

    for phase in range(3):
        for t in range(F):
            for dh, dw in SIDES:
                @pl.when(present(dh, dw))
                def _():
                    copy_to(phase, t, dh, dw).wait_send()


def local(cotangent, stored_first, stored_second, w_first, w_second, w_third):
    F, R, W, C = cotangent.shape
    sizes = (lax.axis_size("ha"), lax.axis_size("wa"), F, R, W, C)
    A, rows = W // NB, W * R // 2
    f32, bf16 = jnp.float32, jnp.bfloat16
    wbuf = pltpu.VMEM(w_first.shape, f32)
    block = pltpu.VMEM((F, R, W, C), f32)
    edge = -(-R // 8) * 8
    return pl.pallas_call(
        functools.partial(kernel, sizes),
        out_shape=pltpu.VMEM(cotangent.shape, jnp.float32),
        in_specs=[pl.BlockSpec(memory_space=pltpu.HBM)] * 6,
        out_specs=pl.BlockSpec(memory_space=pltpu.VMEM),
        scratch_shapes=[
            block, block, block,
            pltpu.VMEM((2, F, 2, rows, LANES), f32),
            wbuf, wbuf, wbuf,
            pltpu.VMEM((3, 3, 4, 2 * LANES, 3 * LANES), bf16),
            pltpu.VMEM((3, F, 2, rows, LANES), f32),
            pltpu.VMEM((F, 4, NB + 2, R // 2 * A, 2 * LANES), bf16),
            pltpu.VMEM((F, 4, rows, LANES), f32),
            pltpu.VMEM((3, F, 2, 3 * A, LANES), f32),
            pltpu.VMEM((3, F, 2, 3 * A, LANES), f32),
            pltpu.VMEM((3, F, 2, edge, LANES), f32),
            pltpu.VMEM((3, F, 2, edge, LANES), f32),
            pltpu.VMEM((3, F, 2, 2, edge, LANES), f32),
            pltpu.SemaphoreType.DMA((6,)),
            pltpu.SemaphoreType.DMA((3, F, 8)),
            pltpu.SemaphoreType.DMA((3, F, 8)),
        ],
        compiler_params=pltpu.CompilerParams(
            collective_id=0, has_side_effects=True,
            vmem_limit_bytes=67043328 - cotangent.size * 6,
        ),
    )(cotangent, stored_first, stored_second, w_first, w_second, w_third)


def solution(mesh):
    split_spec = P("clip", "ha", "wa", None)
    return jax.shard_map(
        local,
        mesh=mesh,
        in_specs=(split_spec, split_spec, split_spec, P(), P(), P()),
        out_specs=split_spec,
        check_vma=False,
    )
```

time: 26.9 us -> 26.8 us (level)
  no operation moved by 1% of the time
where the time goes in v2:
time: 26.8 us; the launch traced here: 26.6 us
  Pallas kernels  25.8 us (96%)
  local copies, waits for them, and re-layouts  0.8 us (3%)
    pallas_call x1, Pallas kernels, local(): pl.pallas_call(functools.partial(kernel, sizes), out_shape=pltpu.VMEM(cot...  25.8 us
    unnamed x1, local copies, waits for them, and re-layouts  0.8 us

profile of v2, /device:TPU:1, one launch (start us, length us, event | category | flops | bytes accessed | tf_op | source)
XLA Modules:
  0.0 26.6 jit_solution(8660837130854098039)
XLA Ops:
  0.0 25.8 %shard_map.64 = f32[4,4,64,96]{3,2,1,0:T(8,128)S(1)} custom-call(f32[4,4,64,96]{3,2,1,0:T(8,128)} %cot.1, f32[4,4,64,96]{3,2,1,0:T(8,128)} %first.1, f32[4,4,64,96]{3,2,1,0:T(8,128)} %second.1, f32[3,3,3,96,96]{4,3,2,1,0:T(8,128)} %w1.1, f32[3,3,3,96,96]{4,3,2,1,0:T(8,128)} %w2.1, f32[3,3,3,96,96]{4,3,2,1,0:T(8,128)} %w3.1), custom_call_target="tpu_custom_call" | custom-call | tf_op jit(solution)/shard_map/pallas_call | solution.py:277
  25.8 0.8 %copy.8 = f32[4,4,64,96]{3,2,1,0:T(8,128)} copy(f32[4,4,64,96]{3,2,1,0:T(8,128)S(1)} %shard_map.64) | data formatting | bytes 786432

commit v3 on v2

--- a/solution.py
+++ b/solution.py
@@ -164,13 +164,16 @@
         @pl.loop(0, 3)
         def _(i):
             for k in range(3):
-                g0, g1, g2 = (wide(wbuf[i, 2 - e, k]) for e in range(3))
+                g0, g1, g2 = (wide(jnp.transpose(wbuf[i, 2 - e, k])) for e in range(3))
                 even, odd = (g0 + g2) * 0.5, g1 * 0.5
                 for q, value in enumerate((g0, even + odd, even - odd, g2)):
                     high, low = split(value)
                     at = k * LANES
-                    wh[phase, i, q, 0:C, at : at + LANES] = high
-                    wh[phase, i, q, LANES : LANES + C, at : at + LANES] = low
+                    wh[phase, i, q, at : at + C, 0:LANES] = high
+                    wh[phase, i, q, at : at + C, LANES:] = low
+                    wh[phase, i, q, at + C : at + LANES, :] = jnp.zeros(
+                        (LANES - C, 2 * LANES), jnp.bfloat16
+                    )
 
     def slope_of(stored, at):
         @pl.loop(0, F)
@@ -219,14 +222,10 @@
         a = jnp.concatenate(
             [lhs[t, q, 2 - k : 2 - k + NB].reshape(rows, 2 * LANES) for k in range(3)], axis=1
         )
-        w = [wh[phase, i, q, :, k * LANES : (k + 1) * LANES] for k in range(3)]
-        b = jnp.concatenate([w[0], w[0], w[1], w[1], w[2], w[2]], axis=1)
-        value = lax.dot_general(
-            a, b, (((1,), (1,)), ((), ())), preferred_element_type=jnp.float32
-        )
+        w = [wh[phase, i, q, k * LANES : (k + 1) * LANES] for k in range(3)]
+        b = jnp.concatenate([w[0], w[0], w[1], w[1], w[2], w[2]], axis=0)
+        value = jnp.dot(a, b, preferred_element_type=jnp.float32)
         return value[:, :LANES] + value[:, LANES:]
-
-    allreal = lax.broadcasted_iota(jnp.int32, (rows, LANES), 1) < C
 
     for phase in range(3):
         for t in reversed(range(F)):
@@ -238,7 +237,7 @@
                 m.append(value if t == F - 1 else value + acc[t, q])
             done = (m[0] + m[1] + m[2], m[1] - m[2] - m[3])
             if phase < 2:
-                done = [jnp.where(allreal, done[s] * slopes[phase, t, s], 0.0) for s in range(2)]
+                done = [done[s] * slopes[phase, t, s] for s in range(2)]
                 for s in range(2):
                     own[phase + 1, t, s] = done[s]
                 post(phase + 1, t, lambda r, b: done[r % 2][place(b, r) : place(b, r) + A])
@@ -283,7 +282,7 @@
             block, block, block,
             pltpu.VMEM((2, F, 2, rows, LANES), f32),
             wbuf, wbuf, wbuf,
-            pltpu.VMEM((3, 3, 4, 2 * LANES, 3 * LANES), bf16),
+            pltpu.VMEM((3, 3, 4, 3 * LANES, 2 * LANES), bf16),
             pltpu.VMEM((3, F, 2, rows, LANES), f32),
             pltpu.VMEM((F, 4, NB + 2, R // 2 * A, 2 * LANES), bf16),
             pltpu.VMEM((F, 4, rows, LANES), f32),

time: 26.8 us -> 21 us (0.78)
  Pallas kernels: 25.8 us -> 20 us
    pallas_call x1, Pallas kernels: 25.8 us -> 20 us  [local(): pl.pallas_call(functools.partial(kernel, sizes), out_shape=pltpu.VMEM(cot...]
where the time goes in v3:
time: 21 us; the launch traced here: 20.8 us
  Pallas kernels  20 us (95%)
  local copies, waits for them, and re-layouts  0.8 us (4%)
    pallas_call x1, Pallas kernels, local(): pl.pallas_call(functools.partial(kernel, sizes), out_shape=pltpu.VMEM(cot...  20 us
    unnamed x1, local copies, waits for them, and re-layouts  0.8 us

profile of v3, /device:TPU:1, one launch (start us, length us, event | category | flops | bytes accessed | tf_op | source)
XLA Modules:
  0.0 20.8 jit_solution(1761582701425711498)
XLA Ops:
  0.0 20.0 %shard_map.64 = f32[4,4,64,96]{3,2,1,0:T(8,128)S(1)} custom-call(f32[4,4,64,96]{3,2,1,0:T(8,128)} %cot.1, f32[4,4,64,96]{3,2,1,0:T(8,128)} %first.1, f32[4,4,64,96]{3,2,1,0:T(8,128)} %second.1, f32[3,3,3,96,96]{4,3,2,1,0:T(8,128)} %w1.1, f32[3,3,3,96,96]{4,3,2,1,0:T(8,128)} %w2.1, f32[3,3,3,96,96]{4,3,2,1,0:T(8,128)} %w3.1), custom_call_target="tpu_custom_call" | custom-call | tf_op jit(solution)/shard_map/pallas_call | solution.py:276
  20.0 0.8 %copy.8 = f32[4,4,64,96]{3,2,1,0:T(8,128)} copy(f32[4,4,64,96]{3,2,1,0:T(8,128)S(1)} %shard_map.64) | data formatting | bytes 786432

commit v4 on v3

--- a/solution.py
+++ b/solution.py
@@ -8,6 +8,7 @@
 from jax.sharding import PartitionSpec as P
 
 LANES = 128
+EDGE = 8
 NB = 4
 SIDES = tuple((dh, dw) for dh in (-1, 0, 1) for dw in (-1, 0, 1) if (dh, dw) != (0, 0))
 CORNERS = tuple(s for s in SIDES if s[0] and s[1])
@@ -30,7 +31,7 @@
 def kernel(
     sizes, cot, first, second, w1, w2, w3, out,
     vcot, sfirst, ssecond, slopes, wbuf0, wbuf1, wbuf2, wh, own, lhs, acc,
-    zsend, zrecv, xsend, xrecv, crecv,
+    zraw, xraw, craw, zsend, zrecv, xsend, xrecv, crecv, rawbytes, bytes_,
     local_sem, send_sem, recv_sem,
 ):
     nh, nw, F, R, W, C = sizes
@@ -74,20 +75,36 @@
         return (d + 1) // 2
 
     def landing(phase, t, dh, dw):
+        if phase == 0:
+            if dh and dw:
+                return craw.at[t, side(dh), side(dw)]
+            if dw:
+                return xraw.at[t, side(dw)]
+            return zraw.at[t, side(dh)]
         if dh and dw:
-            return crecv.at[phase, t, side(dh), side(dw)]
+            return crecv.at[phase - 1, t, side(dh), side(dw)]
         if dw:
-            return xrecv.at[phase, t, side(dw)]
-        return zrecv.at[phase, t, side(dh)]
+            return xrecv.at[phase - 1, t, side(dw)]
+        return zrecv.at[phase - 1, t, side(dh)]
+
+    def source(phase, t, dh, dw):
+        if phase == 0:
+            row = {-1: 0, 0: pl.ds(0, R), 1: R - 1}[dh]
+            col = {-1: pl.ds(0, EDGE), 0: pl.ds(0, W), 1: pl.ds(W - EDGE, EDGE)}[dw]
+            return cot.at[t, row, col, :]
+        if dw:
+            return xsend.at[phase - 1, t, side(dw)]
+        return zsend.at[phase - 1, t, side(dh)]
+
+    def arrival(phase, t):
+        return recv_sem.at[phase % 2, t]
 
     def copy_to(phase, t, dh, dw):
-        at = SIDES.index((dh, dw))
-        source = xsend.at[phase, t, side(dw)] if dw else zsend.at[phase, t, side(dh)]
         return pltpu.make_async_remote_copy(
-            src_ref=source,
+            src_ref=source(phase, t, dh, dw),
             dst_ref=landing(phase, t, -dh, -dw),
-            send_sem=send_sem.at[phase, t, at],
-            recv_sem=recv_sem.at[phase, t, at],
+            send_sem=send_sem.at[min(phase, 1)],
+            recv_sem=arrival(phase, t),
             device_id={"ha": ih + dh, "wa": iw + dw},
             device_id_type=pl.DeviceIdType.MESH,
         )
@@ -98,11 +115,34 @@
             def _():
                 copy_to(phase, t, dh, dw).start()
 
+    def amount(phase, up, across):
+        row = W // EDGE if phase == 0 else 3 * A // EDGE
+        column = R if phase == 0 else xsend.shape[-2] // EDGE
+        corner = 1 if phase == 0 else column
+        return up * row + across * column + up * across * corner
+
+    def by_neighbours(wait):
+        for up in range(3):
+            for across in range(3):
+                if up + across:
+                    @pl.when((tall == up + 1) & (broad == across + 1))
+                    def _():
+                        wait(up, across)
+
     def receive(phase, t):
-        for dh, dw in ORDER:
-            @pl.when(present(-dh, -dw))
-            def _():
-                copy_to(phase, t, dh, dw).wait_recv()
+        room = rawbytes if phase == 0 else bytes_
+
+        def wait(up, across):
+            part = room.at[0, pl.ds(0, amount(phase, up, across))]
+            pltpu.make_async_copy(part, part, arrival(phase, t)).wait()
+
+        by_neighbours(wait)
+
+    tall = 1 + one(ih > 0) + one(ih < nh - 1)
+    broad = 1 + one(iw > 0) + one(iw < nw - 1)
+    pl.semaphore_wait(barrier, tall * broad - 1)
+    for t in reversed(range(F)):
+        send(0, t)
 
     for dh, dw in SIDES:
         @pl.when(jnp.logical_not(present(dh, dw)))
@@ -130,33 +170,18 @@
             last = tile(r, NB - 1)
             for m in range(3):
                 moved = pltpu.roll(last, LANES - third - third * m, axis=1)
-                zsend[phase, t, to, m * A : (m + 1) * A, :] = jnp.where(real, tile(r, m), moved)
+                zsend[phase - 1, t, to, m * A : (m + 1) * A, :] = jnp.where(real, tile(r, m), moved)
         for r in range(R):
-            xsend[phase, t, 0, r : r + 1, :] = tile(r, 0)[0:1]
-            xsend[phase, t, 1, r : r + 1, :] = tile(r, NB - 1)[A - 1 : A]
+            xsend[phase - 1, t, 0, r : r + 1, :] = tile(r, 0)[0:1]
+            xsend[phase - 1, t, 1, r : r + 1, :] = tile(r, NB - 1)[A - 1 : A]
 
     def unpack(phase, t, to):
-        packed = [zrecv[phase, t, to, m * A : (m + 1) * A, :] for m in range(3)]
+        packed = [zrecv[phase - 1, t, to, m * A : (m + 1) * A, :] for m in range(3)]
         moved = [pltpu.roll(packed[m], third + third * m, axis=1) for m in range(3)]
         last = jnp.where(lane < third, moved[0], jnp.where(lane < 2 * third, moved[1], moved[2]))
         return [jnp.where(real, v, 0.0) for v in packed + [last]]
 
     xsend[...] = jnp.zeros_like(xsend)
-    loads[0].wait()
-
-    for t in reversed(range(F)):
-        tiles = {}
-        for r in range(R):
-            for b in range(NB):
-                tiles[r, b] = wide(vcot[t, r, pl.ds(b, A, stride=NB), :])
-                own[0, t, r % 2, place(b, r) : place(b, r) + A, :] = tiles[r, b]
-        post(0, t, lambda r, b: tiles[r, b])
-
-    tall = 1 + one(ih > 0) + one(ih < nh - 1)
-    broad = 1 + one(iw > 0) + one(iw < nw - 1)
-    pl.semaphore_wait(barrier, tall * broad - 1)
-    for t in reversed(range(F)):
-        send(0, t)
 
     def prepare(phase):
         wbuf = wbufs[phase]
@@ -184,6 +209,7 @@
                         silu_slope(stored[t, r, pl.ds(b, A, stride=NB), :])
                     )
 
+    loads[0].wait()
     loads[1].wait()
     prepare(0)
     loads[2].wait()
@@ -198,16 +224,22 @@
     def arrange(phase, t):
         tiles = {}
         for r in range(-1, R + 1):
-            if 0 <= r < R:
+            to = 0 if r < 0 else 1
+            near = R - 1 if r < 0 else 0
+            if phase == 0:
+                rows_ = vcot.at[t, r] if 0 <= r < R else zraw.at[t, to]
                 for b in range(NB):
-                    tiles[r, b] = own[phase, t, r % 2, place(b, r) : place(b, r) + A, :]
-                left, right = (xrecv[phase, t, s, r : r + 1, :] for s in range(2))
+                    tiles[r, b] = wide(rows_[pl.ds(b, A, stride=NB), :])
+                cells = xraw.at[:, :, r] if 0 <= r < R else craw.at[:, to]
+                left, right = wide(cells[t, 0, EDGE - 1 :]), wide(cells[t, 1, 0:1])
+            elif 0 <= r < R:
+                for b in range(NB):
+                    tiles[r, b] = own[phase - 1, t, r % 2, place(b, r) : place(b, r) + A, :]
+                left, right = (xrecv[phase - 1, t, s, r : r + 1, :] for s in range(2))
             else:
-                to = 0 if r < 0 else 1
                 for b, value in enumerate(unpack(phase, t, to)):
                     tiles[r, b] = value
-                near = R - 1 if r < 0 else 0
-                left, right = (crecv[phase, t, to, s, near : near + 1, :] for s in range(2))
+                left, right = (crecv[phase - 1, t, to, s, near : near + 1, :] for s in range(2))
             tiles[r, -1] = jnp.where(line == 0, left, pltpu.roll(tiles[r, NB - 1], 1, axis=0))
             tiles[r, NB] = jnp.where(line == A - 1, right, pltpu.roll(tiles[r, 0], A - 1, axis=0))
         for p in range(pairs):
@@ -235,11 +267,14 @@
             for q in range(4):
                 value = product(phase, t, 2, q)
                 m.append(value if t == F - 1 else value + acc[t, q])
+            if 0 < t < F - 1:
+                for q in range(4):
+                    acc[t - 1, q] = product(phase, t + 1, 0, q)
             done = (m[0] + m[1] + m[2], m[1] - m[2] - m[3])
             if phase < 2:
                 done = [done[s] * slopes[phase, t, s] for s in range(2)]
                 for s in range(2):
-                    own[phase + 1, t, s] = done[s]
+                    own[phase, t, s] = done[s]
                 post(phase + 1, t, lambda r, b: done[r % 2][place(b, r) : place(b, r) + A])
                 send(phase + 1, t)
             else:
@@ -248,21 +283,19 @@
                         out[t, r, pl.ds(b, A, stride=NB), :] = done[r % 2][
                             place(b, r) : place(b, r) + A, :C
                         ]
-            for back in (1, 2):
-                if t - back >= 0:
-                    for q in range(4):
-                        value = product(phase, t, 2 - back, q)
-                        if t + 1 < F and back == 1:
-                            acc[t - 1, q] += value
-                        else:
-                            acc[t - back, q] = value
-
-    for phase in range(3):
-        for t in range(F):
-            for dh, dw in SIDES:
-                @pl.when(present(dh, dw))
-                def _():
-                    copy_to(phase, t, dh, dw).wait_send()
+            if t > 0:
+                for q in range(4):
+                    value = product(phase, t, 1, q)
+                    acc[t - 1, q] = value if t == F - 1 else value + acc[t - 1, q]
+
+    def sent(up, across):
+        part = rawbytes.at[:, pl.ds(0, amount(0, up, across))]
+        pltpu.make_async_copy(part, part, send_sem.at[0]).wait()
+        part = bytes_.at[:, pl.ds(0, amount(1, up, across))]
+        for _ in range(2):
+            pltpu.make_async_copy(part, part, send_sem.at[1]).wait()
+
+    by_neighbours(sent)
 
 
 def local(cotangent, stored_first, stored_second, w_first, w_second, w_third):
@@ -272,7 +305,7 @@
     f32, bf16 = jnp.float32, jnp.bfloat16
     wbuf = pltpu.VMEM(w_first.shape, f32)
     block = pltpu.VMEM((F, R, W, C), f32)
-    edge = -(-R // 8) * 8
+    edge = -(-R // EDGE) * EDGE
     return pl.pallas_call(
         functools.partial(kernel, sizes),
         out_shape=pltpu.VMEM(cotangent.shape, jnp.float32),
@@ -283,17 +316,22 @@
             pltpu.VMEM((2, F, 2, rows, LANES), f32),
             wbuf, wbuf, wbuf,
             pltpu.VMEM((3, 3, 4, 3 * LANES, 2 * LANES), bf16),
-            pltpu.VMEM((3, F, 2, rows, LANES), f32),
+            pltpu.VMEM((2, F, 2, rows, LANES), f32),
             pltpu.VMEM((F, 4, NB + 2, R // 2 * A, 2 * LANES), bf16),
             pltpu.VMEM((F, 4, rows, LANES), f32),
-            pltpu.VMEM((3, F, 2, 3 * A, LANES), f32),
-            pltpu.VMEM((3, F, 2, 3 * A, LANES), f32),
-            pltpu.VMEM((3, F, 2, edge, LANES), f32),
-            pltpu.VMEM((3, F, 2, edge, LANES), f32),
-            pltpu.VMEM((3, F, 2, 2, edge, LANES), f32),
+            pltpu.VMEM((F, 2, W, C), f32),
+            pltpu.VMEM((F, 2, R, EDGE, C), f32),
+            pltpu.VMEM((F, 2, 2, EDGE, C), f32),
+            pltpu.VMEM((2, F, 2, 3 * A, LANES), f32),
+            pltpu.VMEM((2, F, 2, 3 * A, LANES), f32),
+            pltpu.VMEM((2, F, 2, edge, LANES), f32),
+            pltpu.VMEM((2, F, 2, edge, LANES), f32),
+            pltpu.VMEM((2, F, 2, 2, edge, LANES), f32),
+            pltpu.VMEM((F, 2 * W // EDGE + 2 * R + 4, EDGE, C), f32),
+            pltpu.VMEM((F, 6 * A // EDGE + 6 * edge // EDGE, EDGE, LANES), f32),
             pltpu.SemaphoreType.DMA((6,)),
-            pltpu.SemaphoreType.DMA((3, F, 8)),
-            pltpu.SemaphoreType.DMA((3, F, 8)),
+            pltpu.SemaphoreType.DMA((2,)),
+            pltpu.SemaphoreType.DMA((2, F)),
         ],
         compiler_params=pltpu.CompilerParams(
             collective_id=0, has_side_effects=True,

time: 21 us -> 19.1 us (0.910)
  Pallas kernels: 20 us -> 18.1 us
    pallas_call x1, Pallas kernels: 20 us -> 18.1 us  [local(): pl.pallas_call(functools.partial(kernel, sizes), out_shape=pltpu.VMEM(cot...]
where the time goes in v4:
time: 19.1 us; the launch traced here: 18.9 us
  Pallas kernels  18.1 us (95%)
  local copies, waits for them, and re-layouts  0.8 us (4%)
    pallas_call x1, Pallas kernels, local(): pl.pallas_call(functools.partial(kernel, sizes), out_shape=pltpu.VMEM(cot...  18.1 us
    unnamed x1, local copies, waits for them, and re-layouts  0.8 us

profile of v4, /device:TPU:1, one launch (start us, length us, event | category | flops | bytes accessed | tf_op | source)
XLA Modules:
  0.0 18.9 jit_solution(234622150587642802)
XLA Ops:
  0.0 18.1 %shard_map.64 = f32[4,4,64,96]{3,2,1,0:T(8,128)S(1)} custom-call(f32[4,4,64,96]{3,2,1,0:T(8,128)} %cot.1, f32[4,4,64,96]{3,2,1,0:T(8,128)} %first.1, f32[4,4,64,96]{3,2,1,0:T(8,128)} %second.1, f32[3,3,3,96,96]{4,3,2,1,0:T(8,128)} %w1.1, f32[3,3,3,96,96]{4,3,2,1,0:T(8,128)} %w2.1, f32[3,3,3,96,96]{4,3,2,1,0:T(8,128)} %w3.1), custom_call_target="tpu_custom_call" | custom-call | tf_op jit(solution)/shard_map/pallas_call | solution.py:309
  18.1 0.8 %copy.8 = f32[4,4,64,96]{3,2,1,0:T(8,128)} copy(f32[4,4,64,96]{3,2,1,0:T(8,128)S(1)} %shard_map.64) | data formatting | bytes 786432

commit v5 on v3

--- a/solution.py
+++ b/solution.py
@@ -8,6 +8,7 @@
 from jax.sharding import PartitionSpec as P
 
 LANES = 128
+EDGE = 8
 NB = 4
 SIDES = tuple((dh, dw) for dh in (-1, 0, 1) for dw in (-1, 0, 1) if (dh, dw) != (0, 0))
 CORNERS = tuple(s for s in SIDES if s[0] and s[1])
@@ -30,7 +31,7 @@
 def kernel(
     sizes, cot, first, second, w1, w2, w3, out,
     vcot, sfirst, ssecond, slopes, wbuf0, wbuf1, wbuf2, wh, own, lhs, acc,
-    zsend, zrecv, xsend, xrecv, crecv,
+    zsend, zrecv, xsend, xrecv, crecv, room,
     local_sem, send_sem, recv_sem,
 ):
     nh, nw, F, R, W, C = sizes
@@ -67,8 +68,7 @@
         pltpu.make_async_copy(first, sfirst, local_sem.at[5]),
         pltpu.make_async_copy(w1, wbuf2, local_sem.at[3]),
     ]
-    for load in loads:
-        load.start()
+    loads[0].start()
 
     def side(d):
         return (d + 1) // 2
@@ -80,14 +80,15 @@
             return xrecv.at[phase, t, side(dw)]
         return zrecv.at[phase, t, side(dh)]
 
+    def arrival(phase, t):
+        return recv_sem.at[phase % 2, t]
+
     def copy_to(phase, t, dh, dw):
-        at = SIDES.index((dh, dw))
-        source = xsend.at[phase, t, side(dw)] if dw else zsend.at[phase, t, side(dh)]
         return pltpu.make_async_remote_copy(
-            src_ref=source,
+            src_ref=xsend.at[phase, t, side(dw)] if dw else zsend.at[phase, t, side(dh)],
             dst_ref=landing(phase, t, -dh, -dw),
-            send_sem=send_sem.at[phase, t, at],
-            recv_sem=recv_sem.at[phase, t, at],
+            send_sem=send_sem.at[0],
+            recv_sem=arrival(phase, t),
             device_id={"ha": ih + dh, "wa": iw + dw},
             device_id_type=pl.DeviceIdType.MESH,
         )
@@ -98,11 +99,27 @@
             def _():
                 copy_to(phase, t, dh, dw).start()
 
+    def amount(up, across):
+        edge = xsend.shape[-2]
+        return up * 3 * A + across * edge + up * across * edge
+
+    def by_neighbours(wait):
+        for up in range(3):
+            for across in range(3):
+                if up + across:
+                    @pl.when((tall == up + 1) & (broad == across + 1))
+                    def _():
+                        wait(up, across)
+
     def receive(phase, t):
-        for dh, dw in ORDER:
-            @pl.when(present(-dh, -dw))
-            def _():
-                copy_to(phase, t, dh, dw).wait_recv()
+        def wait(up, across):
+            part = room.at[0, 0, pl.ds(0, amount(up, across))]
+            pltpu.make_async_copy(part, part, arrival(phase, t)).wait()
+
+        by_neighbours(wait)
+
+    tall = 1 + one(ih > 0) + one(ih < nh - 1)
+    broad = 1 + one(iw > 0) + one(iw < nw - 1)
 
     for dh, dw in SIDES:
         @pl.when(jnp.logical_not(present(dh, dw)))
@@ -143,6 +160,8 @@
 
     xsend[...] = jnp.zeros_like(xsend)
     loads[0].wait()
+    for load in loads[1:]:
+        load.start()
 
     for t in reversed(range(F)):
         tiles = {}
@@ -152,8 +171,6 @@
                 own[0, t, r % 2, place(b, r) : place(b, r) + A, :] = tiles[r, b]
         post(0, t, lambda r, b: tiles[r, b])
 
-    tall = 1 + one(ih > 0) + one(ih < nh - 1)
-    broad = 1 + one(iw > 0) + one(iw < nw - 1)
     pl.semaphore_wait(barrier, tall * broad - 1)
     for t in reversed(range(F)):
         send(0, t)
@@ -198,15 +215,15 @@
     def arrange(phase, t):
         tiles = {}
         for r in range(-1, R + 1):
+            to = 0 if r < 0 else 1
+            near = R - 1 if r < 0 else 0
             if 0 <= r < R:
                 for b in range(NB):
                     tiles[r, b] = own[phase, t, r % 2, place(b, r) : place(b, r) + A, :]
                 left, right = (xrecv[phase, t, s, r : r + 1, :] for s in range(2))
             else:
-                to = 0 if r < 0 else 1
                 for b, value in enumerate(unpack(phase, t, to)):
                     tiles[r, b] = value
-                near = R - 1 if r < 0 else 0
                 left, right = (crecv[phase, t, to, s, near : near + 1, :] for s in range(2))
             tiles[r, -1] = jnp.where(line == 0, left, pltpu.roll(tiles[r, NB - 1], 1, axis=0))
             tiles[r, NB] = jnp.where(line == A - 1, right, pltpu.roll(tiles[r, 0], A - 1, axis=0))
@@ -218,23 +235,29 @@
                     lhs[t, q, b + 1, p * A : (p + 1) * A, 0:LANES] = high
                     lhs[t, q, b + 1, p * A : (p + 1) * A, LANES:] = low
 
-    def product(phase, t, i, q):
-        a = jnp.concatenate(
-            [lhs[t, q, 2 - k : 2 - k + NB].reshape(rows, 2 * LANES) for k in range(3)], axis=1
+    def product(phase, t, q, taps):
+        a, b = [], []
+        for i in taps:
+            for k in range(3):
+                part = lhs[t + 2 - i, q, 2 - k : 2 - k + NB]
+                a.append(part.reshape(rows, 2 * LANES))
+                b += [wh[phase, i, q, k * LANES : (k + 1) * LANES]] * 2
+        value = jnp.dot(
+            jnp.concatenate(a, axis=1), jnp.concatenate(b, axis=0),
+            preferred_element_type=jnp.float32,
         )
-        w = [wh[phase, i, q, k * LANES : (k + 1) * LANES] for k in range(3)]
-        b = jnp.concatenate([w[0], w[0], w[1], w[1], w[2], w[2]], axis=0)
-        value = jnp.dot(a, b, preferred_element_type=jnp.float32)
         return value[:, :LANES] + value[:, LANES:]
 
+    ahead = (False, True, True)
     for phase in range(3):
         for t in reversed(range(F)):
             receive(phase, t)
             arrange(phase, t)
-            m = []
-            for q in range(4):
-                value = product(phase, t, 2, q)
-                m.append(value if t == F - 1 else value + acc[t, q])
+            older = range(max(0, t + 3 - F), 2)
+            if ahead[phase] and older:
+                m = [product(phase, t, q, (2,)) + acc[q] for q in range(4)]
+            else:
+                m = [product(phase, t, q, (*older, 2)) for q in range(4)]
             done = (m[0] + m[1] + m[2], m[1] - m[2] - m[3])
             if phase < 2:
                 done = [done[s] * slopes[phase, t, s] for s in range(2)]
@@ -248,21 +271,15 @@
                         out[t, r, pl.ds(b, A, stride=NB), :] = done[r % 2][
                             place(b, r) : place(b, r) + A, :C
                         ]
-            for back in (1, 2):
-                if t - back >= 0:
-                    for q in range(4):
-                        value = product(phase, t, 2 - back, q)
-                        if t + 1 < F and back == 1:
-                            acc[t - 1, q] += value
-                        else:
-                            acc[t - back, q] = value
-
-    for phase in range(3):
-        for t in range(F):
-            for dh, dw in SIDES:
-                @pl.when(present(dh, dw))
-                def _():
-                    copy_to(phase, t, dh, dw).wait_send()
+            if ahead[phase] and t > 0:
+                for q in range(4):
+                    acc[q] = product(phase, t - 1, q, range(max(0, t + 2 - F), 2))
+
+    def sent(up, across):
+        part = room.at[:, :, pl.ds(0, amount(up, across))]
+        pltpu.make_async_copy(part, part, send_sem.at[0]).wait()
+
+    by_neighbours(sent)
 
 
 def local(cotangent, stored_first, stored_second, w_first, w_second, w_third):
@@ -272,7 +289,7 @@
     f32, bf16 = jnp.float32, jnp.bfloat16
     wbuf = pltpu.VMEM(w_first.shape, f32)
     block = pltpu.VMEM((F, R, W, C), f32)
-    edge = -(-R // 8) * 8
+    edge = -(-R // EDGE) * EDGE
     return pl.pallas_call(
         functools.partial(kernel, sizes),
         out_shape=pltpu.VMEM(cotangent.shape, jnp.float32),
@@ -285,15 +302,16 @@
             pltpu.VMEM((3, 3, 4, 3 * LANES, 2 * LANES), bf16),
             pltpu.VMEM((3, F, 2, rows, LANES), f32),
             pltpu.VMEM((F, 4, NB + 2, R // 2 * A, 2 * LANES), bf16),
-            pltpu.VMEM((F, 4, rows, LANES), f32),
+            pltpu.VMEM((4, rows, LANES), f32),
             pltpu.VMEM((3, F, 2, 3 * A, LANES), f32),
             pltpu.VMEM((3, F, 2, 3 * A, LANES), f32),
             pltpu.VMEM((3, F, 2, edge, LANES), f32),
             pltpu.VMEM((3, F, 2, edge, LANES), f32),
             pltpu.VMEM((3, F, 2, 2, edge, LANES), f32),
+            pltpu.VMEM((3, F, 6 * A + 6 * edge, LANES), f32),
             pltpu.SemaphoreType.DMA((6,)),
-            pltpu.SemaphoreType.DMA((3, F, 8)),
-            pltpu.SemaphoreType.DMA((3, F, 8)),
+            pltpu.SemaphoreType.DMA((1,)),
+            pltpu.SemaphoreType.DMA((2, F)),
         ],
         compiler_params=pltpu.CompilerParams(
             collective_id=0, has_side_effects=True,

time: 21 us -> 19.1 us (0.910)
  Pallas kernels: 20 us -> 18 us
    pallas_call x1, Pallas kernels: 20 us -> 18 us  [local(): pl.pallas_call(functools.partial(kernel, sizes), out_shape=pltpu.VMEM(cot...]
where the time goes in v5:
time: 19.1 us; the launch traced here: 18.8 us
  Pallas kernels  18 us (94%)
  local copies, waits for them, and re-layouts  0.8 us (4%)
    pallas_call x1, Pallas kernels, local(): pl.pallas_call(functools.partial(kernel, sizes), out_shape=pltpu.VMEM(cot...  18 us
    unnamed x1, local copies, waits for them, and re-layouts  0.8 us

profile of v5, /device:TPU:1, one launch (start us, length us, event | category | flops | bytes accessed | tf_op | source)
XLA Modules:
  0.0 18.8 jit_solution(7841198266243331801)
XLA Ops:
  0.0 18.0 %shard_map.64 = f32[4,4,64,96]{3,2,1,0:T(8,128)S(1)} custom-call(f32[4,4,64,96]{3,2,1,0:T(8,128)} %cot.1, f32[4,4,64,96]{3,2,1,0:T(8,128)} %first.1, f32[4,4,64,96]{3,2,1,0:T(8,128)} %second.1, f32[3,3,3,96,96]{4,3,2,1,0:T(8,128)} %w1.1, f32[3,3,3,96,96]{4,3,2,1,0:T(8,128)} %w2.1, f32[3,3,3,96,96]{4,3,2,1,0:T(8,128)} %w3.1), custom_call_target="tpu_custom_call" | custom-call | tf_op jit(solution)/shard_map/pallas_call | solution.py:293
  18.0 0.8 %copy.8 = f32[4,4,64,96]{3,2,1,0:T(8,128)} copy(f32[4,4,64,96]{3,2,1,0:T(8,128)S(1)} %shard_map.64) | data formatting | bytes 786432

commit v6 on v5

--- a/solution.py
+++ b/solution.py
@@ -30,7 +30,7 @@
 
 def kernel(
     sizes, cot, first, second, w1, w2, w3, out,
-    vcot, sfirst, ssecond, slopes, wbuf0, wbuf1, wbuf2, wh, own, lhs, acc,
+    vcot, sfirst, ssecond, wbuf0, wbuf1, wbuf2, wh, own, lhs, acc,
     zsend, zrecv, xsend, xrecv, crecv, room,
     local_sem, send_sem, recv_sem,
 ):
@@ -61,14 +61,25 @@
             )
 
     loads = [
-        pltpu.make_async_copy(cot, vcot, local_sem.at[0]),
+        pltpu.make_async_copy(
+            cot.at[:, pl.ds(1, R - 2), pl.ds(EDGE, W - 2 * EDGE)],
+            vcot.at[:, pl.ds(1, R - 2), pl.ds(EDGE, W - 2 * EDGE)], local_sem.at[0],
+        ),
         pltpu.make_async_copy(w3, wbuf0, local_sem.at[1]),
         pltpu.make_async_copy(second, ssecond, local_sem.at[4]),
         pltpu.make_async_copy(w2, wbuf1, local_sem.at[2]),
         pltpu.make_async_copy(first, sfirst, local_sem.at[5]),
         pltpu.make_async_copy(w1, wbuf2, local_sem.at[3]),
     ]
-    loads[0].start()
+    rim = [
+        pltpu.make_async_copy(cot.at[:, r, c], vcot.at[:, r, c], local_sem.at[6 + n])
+        for n, (r, c) in enumerate((
+            (0, pl.ds(0, W)), (R - 1, pl.ds(0, W)),
+            (pl.ds(1, R - 2), pl.ds(0, EDGE)), (pl.ds(1, R - 2), pl.ds(W - EDGE, EDGE)),
+        ))
+    ]
+    for load in rim:
+        load.start()
 
     def side(d):
         return (d + 1) // 2
@@ -142,15 +153,20 @@
     def place(b, r):
         return (b * pairs + r // 2) * A
 
-    def post(phase, t, tile):
+    def post(phase, t, tile, cell=None):
+        if cell is None:
+            def cell(r, w):
+                a = w // NB
+                return tile(r, w % NB)[a : a + 1]
+
         for r, to in ((0, 0), (R - 1, 1)):
             last = tile(r, NB - 1)
             for m in range(3):
                 moved = pltpu.roll(last, LANES - third - third * m, axis=1)
                 zsend[phase, t, to, m * A : (m + 1) * A, :] = jnp.where(real, tile(r, m), moved)
         for r in range(R):
-            xsend[phase, t, 0, r : r + 1, :] = tile(r, 0)[0:1]
-            xsend[phase, t, 1, r : r + 1, :] = tile(r, NB - 1)[A - 1 : A]
+            xsend[phase, t, 0, r : r + 1, :] = cell(r, 0)
+            xsend[phase, t, 1, r : r + 1, :] = cell(r, W - 1)
 
     def unpack(phase, t, to):
         packed = [zrecv[phase, t, to, m * A : (m + 1) * A, :] for m in range(3)]
@@ -159,58 +175,51 @@
         return [jnp.where(real, v, 0.0) for v in packed + [last]]
 
     xsend[...] = jnp.zeros_like(xsend)
+    for load in rim:
+        load.wait()
+    for load in loads:
+        load.start()
+
+    def given(t, r, b):
+        return wide(vcot[t, r, pl.ds(b, A, stride=NB), :])
+
+    def given_cell(t, r, w):
+        return wide(vcot[t, r, w : w + 1, :])
+
+    post(0, F - 1, functools.partial(given, F - 1), functools.partial(given_cell, F - 1))
+    pl.semaphore_wait(barrier, tall * broad - 1)
+    send(0, F - 1)
+    for t in reversed(range(F - 1)):
+        post(0, t, functools.partial(given, t), functools.partial(given_cell, t))
+        send(0, t)
+
+    def prepare(phase, i):
+        for k in range(3):
+            g0, g1, g2 = (wide(jnp.transpose(wbufs[phase][i, 2 - e, k])) for e in range(3))
+            even, odd = (g0 + g2) * 0.5, g1 * 0.5
+            for q, value in enumerate((g0, even + odd, even - odd, g2)):
+                high, low = split(value)
+                at = k * LANES
+                wh[phase, i, q, at : at + C, 0:LANES] = high
+                wh[phase, i, q, at : at + C, LANES:] = low
+                wh[phase, i, q, at + C : at + LANES, :] = jnp.zeros(
+                    (LANES - C, 2 * LANES), jnp.bfloat16
+                )
+
+    def slope_of(stored, t, s):
+        order = [(b, r) for b in range(NB) for r in range(s, R, 2)]
+        values = [wide(stored[t, r, pl.ds(b, A, stride=NB), :]) for b, r in order]
+        return jnp.concatenate([silu_slope(value) for value in values], axis=0)
+
     loads[0].wait()
-    for load in loads[1:]:
-        load.start()
-
-    for t in reversed(range(F)):
-        tiles = {}
-        for r in range(R):
-            for b in range(NB):
-                tiles[r, b] = wide(vcot[t, r, pl.ds(b, A, stride=NB), :])
-                own[0, t, r % 2, place(b, r) : place(b, r) + A, :] = tiles[r, b]
-        post(0, t, lambda r, b: tiles[r, b])
-
-    pl.semaphore_wait(barrier, tall * broad - 1)
-    for t in reversed(range(F)):
-        send(0, t)
-
-    def prepare(phase):
-        wbuf = wbufs[phase]
-
-        @pl.loop(0, 3)
-        def _(i):
-            for k in range(3):
-                g0, g1, g2 = (wide(jnp.transpose(wbuf[i, 2 - e, k])) for e in range(3))
-                even, odd = (g0 + g2) * 0.5, g1 * 0.5
-                for q, value in enumerate((g0, even + odd, even - odd, g2)):
-                    high, low = split(value)
-                    at = k * LANES
-                    wh[phase, i, q, at : at + C, 0:LANES] = high
-                    wh[phase, i, q, at : at + C, LANES:] = low
-                    wh[phase, i, q, at + C : at + LANES, :] = jnp.zeros(
-                        (LANES - C, 2 * LANES), jnp.bfloat16
-                    )
-
-    def slope_of(stored, at):
-        @pl.loop(0, F)
-        def _(t):
-            for r in range(R):
-                for b in range(NB):
-                    slopes[at, t, r % 2, place(b, r) : place(b, r) + A, :] = wide(
-                        silu_slope(stored[t, r, pl.ds(b, A, stride=NB), :])
-                    )
-
     loads[1].wait()
-    prepare(0)
-    loads[2].wait()
-    slope_of(ssecond, 0)
-    loads[3].wait()
-    prepare(1)
-    loads[4].wait()
-    slope_of(sfirst, 1)
-    loads[5].wait()
-    prepare(2)
+
+    @pl.loop(0, 3)
+    def _(i):
+        prepare(0, i)
+
+    for load in loads[2:]:
+        load.wait()
 
     def arrange(phase, t):
         tiles = {}
@@ -219,7 +228,8 @@
             near = R - 1 if r < 0 else 0
             if 0 <= r < R:
                 for b in range(NB):
-                    tiles[r, b] = own[phase, t, r % 2, place(b, r) : place(b, r) + A, :]
+                    at = place(b, r)
+                    tiles[r, b] = own[phase - 1, t, r % 2, at : at + A, :] if phase else given(t, r, b)
                 left, right = (xrecv[phase, t, s, r : r + 1, :] for s in range(2))
             else:
                 for b, value in enumerate(unpack(phase, t, to)):
@@ -248,21 +258,27 @@
         )
         return value[:, :LANES] + value[:, LANES:]
 
-    ahead = (False, True, True)
+    def ahead(phase, t):
+        older = range(max(0, t + 3 - F), 2)
+        return tuple(i for i in older if phase == 2 or (phase == 1 and (t == 2 or (t == 1 and i == 0))))
+
     for phase in range(3):
         for t in reversed(range(F)):
             receive(phase, t)
             arrange(phase, t)
-            older = range(max(0, t + 3 - F), 2)
-            if ahead[phase] and older:
-                m = [product(phase, t, q, (2,)) + acc[q] for q in range(4)]
-            else:
-                m = [product(phase, t, q, (*older, 2)) for q in range(4)]
+            if phase < 2 and t < 3:
+                prepare(phase + 1, t)
+            early = ahead(phase, t)
+            late = [i for i in range(max(0, t + 3 - F), 3) if i not in early]
+            m = [product(phase, t, q, late) for q in range(4)]
+            if early:
+                m = [m[q] + acc[q] for q in range(4)]
             done = (m[0] + m[1] + m[2], m[1] - m[2] - m[3])
             if phase < 2:
-                done = [done[s] * slopes[phase, t, s] for s in range(2)]
+                stored = (ssecond, sfirst)[phase]
+                done = [done[s] * slope_of(stored, t, s) for s in range(2)]
                 for s in range(2):
-                    own[phase + 1, t, s] = done[s]
+                    own[phase, t, s] = done[s]
                 post(phase + 1, t, lambda r, b: done[r % 2][place(b, r) : place(b, r) + A])
                 send(phase + 1, t)
             else:
@@ -271,9 +287,9 @@
                         out[t, r, pl.ds(b, A, stride=NB), :] = done[r % 2][
                             place(b, r) : place(b, r) + A, :C
                         ]
-            if ahead[phase] and t > 0:
+            if t > 0 and ahead(phase, t - 1):
                 for q in range(4):
-                    acc[q] = product(phase, t - 1, q, range(max(0, t + 2 - F), 2))
+                    acc[q] = product(phase, t - 1, q, ahead(phase, t - 1))
 
     def sent(up, across):
         part = room.at[:, :, pl.ds(0, amount(up, across))]
@@ -297,10 +313,9 @@
         out_specs=pl.BlockSpec(memory_space=pltpu.VMEM),
         scratch_shapes=[
             block, block, block,
-            pltpu.VMEM((2, F, 2, rows, LANES), f32),
             wbuf, wbuf, wbuf,
             pltpu.VMEM((3, 3, 4, 3 * LANES, 2 * LANES), bf16),
-            pltpu.VMEM((3, F, 2, rows, LANES), f32),
+            pltpu.VMEM((2, F, 2, rows, LANES), f32),
             pltpu.VMEM((F, 4, NB + 2, R // 2 * A, 2 * LANES), bf16),
             pltpu.VMEM((4, rows, LANES), f32),
             pltpu.VMEM((3, F, 2, 3 * A, LANES), f32),
@@ -309,7 +324,7 @@
             pltpu.VMEM((3, F, 2, edge, LANES), f32),
             pltpu.VMEM((3, F, 2, 2, edge, LANES), f32),
             pltpu.VMEM((3, F, 6 * A + 6 * edge, LANES), f32),
-            pltpu.SemaphoreType.DMA((6,)),
+            pltpu.SemaphoreType.DMA((10,)),
             pltpu.SemaphoreType.DMA((1,)),
             pltpu.SemaphoreType.DMA((2, F)),
         ],

time: 19.1 us -> 19 us (level)
  no operation moved by 1% of the time
where the time goes in v6:
time: 19 us; the launch traced here: 18.8 us
  Pallas kernels  18 us (95%)
  local copies, waits for them, and re-layouts  0.8 us (4%)
    pallas_call x1, Pallas kernels, local(): pl.pallas_call(functools.partial(kernel, sizes), out_shape=pltpu.VMEM(cot...  18 us
    unnamed x1, local copies, waits for them, and re-layouts  0.8 us

profile of v6, /device:TPU:1, one launch (start us, length us, event | category | flops | bytes accessed | tf_op | source)
XLA Modules:
  0.0 18.8 jit_solution(299702045118359048)
XLA Ops:
  0.0 18.0 %shard_map.64 = f32[4,4,64,96]{3,2,1,0:T(8,128)S(1)} custom-call(f32[4,4,64,96]{3,2,1,0:T(8,128)} %cot.1, f32[4,4,64,96]{3,2,1,0:T(8,128)} %first.1, f32[4,4,64,96]{3,2,1,0:T(8,128)} %second.1, f32[3,3,3,96,96]{4,3,2,1,0:T(8,128)} %w1.1, f32[3,3,3,96,96]{4,3,2,1,0:T(8,128)} %w2.1, f32[3,3,3,96,96]{4,3,2,1,0:T(8,128)} %w3.1), custom_call_target="tpu_custom_call" | custom-call | tf_op jit(solution)/shard_map/pallas_call | solution.py:309
  18.1 0.8 %copy.8 = f32[4,4,64,96]{3,2,1,0:T(8,128)} copy(f32[4,4,64,96]{3,2,1,0:T(8,128)S(1)} %shard_map.64) | data formatting | bytes 786432

commit v7 on v6

--- a/solution.py
+++ b/solution.py
@@ -30,7 +30,7 @@
 
 def kernel(
     sizes, cot, first, second, w1, w2, w3, out,
-    vcot, sfirst, ssecond, wbuf0, wbuf1, wbuf2, wh, own, lhs, acc,
+    vcot, sfirst, ssecond, wbuf0, wbuf1, wbuf2, wh, own, lhs, acc, slopes,
     zsend, zrecv, xsend, xrecv, crecv, room,
     local_sem, send_sem, recv_sem,
 ):
@@ -220,6 +220,8 @@
 
     for load in loads[2:]:
         load.wait()
+    for s in range(2):
+        slopes[F - 1, s] = slope_of(ssecond, F - 1, s)
 
     def arrange(phase, t):
         tiles = {}
@@ -276,7 +278,7 @@
             done = (m[0] + m[1] + m[2], m[1] - m[2] - m[3])
             if phase < 2:
                 stored = (ssecond, sfirst)[phase]
-                done = [done[s] * slope_of(stored, t, s) for s in range(2)]
+                done = [done[s] * slopes[t, s] for s in range(2)]
                 for s in range(2):
                     own[phase, t, s] = done[s]
                 post(phase + 1, t, lambda r, b: done[r % 2][place(b, r) : place(b, r) + A])
@@ -287,6 +289,11 @@
                         out[t, r, pl.ds(b, A, stride=NB), :] = done[r % 2][
                             place(b, r) : place(b, r) + A, :C
                         ]
+            if phase < 2:
+                stored, n = (ssecond, t - 1) if t > 0 and phase == 0 else (sfirst, (t - 1) % F)
+                if phase == 0 or t > 0:
+                    for s in range(2):
+                        slopes[n, s] = slope_of(stored, n, s)
             if t > 0 and ahead(phase, t - 1):
                 for q in range(4):
                     acc[q] = product(phase, t - 1, q, ahead(phase, t - 1))
@@ -318,6 +325,7 @@
             pltpu.VMEM((2, F, 2, rows, LANES), f32),
             pltpu.VMEM((F, 4, NB + 2, R // 2 * A, 2 * LANES), bf16),
             pltpu.VMEM((4, rows, LANES), f32),
+            pltpu.VMEM((F, 2, rows, LANES), f32),
             pltpu.VMEM((3, F, 2, 3 * A, LANES), f32),
             pltpu.VMEM((3, F, 2, 3 * A, LANES), f32),
             pltpu.VMEM((3, F, 2, edge, LANES), f32),

time: 19 us -> 19 us (level)
  no operation moved by 1% of the time
where the time goes in v7:
time: 19 us; the launch traced here: 18.8 us
  Pallas kernels  18 us (95%)
  local copies, waits for them, and re-layouts  0.8 us (4%)
    pallas_call x1, Pallas kernels, local(): pl.pallas_call(functools.partial(kernel, sizes), out_shape=pltpu.VMEM(cot...  18 us
    unnamed x1, local copies, waits for them, and re-layouts  0.8 us

profile of v7, /device:TPU:1, one launch (start us, length us, event | category | flops | bytes accessed | tf_op | source)
XLA Modules:
  0.0 18.8 jit_solution(3452388046187451847)
XLA Ops:
  0.0 18.0 %shard_map.64 = f32[4,4,64,96]{3,2,1,0:T(8,128)S(1)} custom-call(f32[4,4,64,96]{3,2,1,0:T(8,128)} %cot.1, f32[4,4,64,96]{3,2,1,0:T(8,128)} %first.1, f32[4,4,64,96]{3,2,1,0:T(8,128)} %second.1, f32[3,3,3,96,96]{4,3,2,1,0:T(8,128)} %w1.1, f32[3,3,3,96,96]{4,3,2,1,0:T(8,128)} %w2.1, f32[3,3,3,96,96]{4,3,2,1,0:T(8,128)} %w3.1), custom_call_target="tpu_custom_call" | custom-call | tf_op jit(solution)/shard_map/pallas_call | solution.py:316
  18.0 0.8 %copy.8 = f32[4,4,64,96]{3,2,1,0:T(8,128)} copy(f32[4,4,64,96]{3,2,1,0:T(8,128)S(1)} %shard_map.64) | data formatting | bytes 786432
